TPU v7x, 32 devices: a whole 2x2x4 slice. The times are simulated.
32 devices in a mesh: gx: 8 (over z, x), gy: 4 (over y, core).
Axes of the slice: x: 2, y: 2, z: 4, core: 2. Of those that a mesh axis runs over, the one named last changes fastest.
Arguments:
- initial_guess_field: float32 [2, 2, 512, 2048], P(None, None, 'gx', 'gy'), may hold values from -18 to 18
- medium_label: int32 [512, 2048], P('gx', 'gy'), may hold values from 0 to 3
- principal_entry_addend: float32 [4, 2], replicated, may hold values from -0.5 to 0.8, as said below
- linearized_block_weight: float32 [25, 4, 2], replicated, may hold values from -1.25 to 1.25
- sample_abscissae: float32 [24, 2], replicated, may hold values from -1 to 1
- singularity_locations: float32 [24, 2], replicated, may hold values from -1 to 6, as said below
- basis_normalizers: float32 [24], replicated, may hold values from 0.8 to 1.6
- spectral_target: float32 [2], replicated, may hold values from -0.5 to 0.5
- quasi_periodic_phase: float32 [2, 2], replicated, may hold values from -3.140625 to 3.140625
Outputs:
- basis: float32 [2, 3, 2, 512, 2048], P(None, None, None, 'gx', 'gy')
- hessenberg: float32 [2, 2, 4, 3], replicated
Inputs may be any that keep to these rules, and one draw needn't show every extreme that they name: `principal_entry_addend`: real parts lie in 0.2 to 0.8, imaginary parts in -0.5 to 0.5. `singularity_locations`: real parts lie in 3 to 6, imaginary parts in -1 to 1.
All inputs are finite; a program needn't handle non-finite values.
Results may differ from a plain program's by a relative error of at most 0.0003.
Values sent between devices are 32-bit elements; how exact they have to be, the bound alone decides.
No kernel may reach another device: no remote copies, remote signals or barrier semaphores. Data moves between devices by JAX's collectives and lax.ppermute only.
A program may use at most 128 MiB of HBM per device.

v0:
```python
import jax
import jax.numpy as jnp
from jax import lax
from jax.sharding import PartitionSpec as P

STEPS = 3
SWEEPS = 4
HIGHEST = lax.Precision.HIGHEST


def padded_2(block, sides, width):
    for axis, dim in sides:
        count = lax.axis_size(axis)
        forward = [(i, i + 1) for i in range(count - 1)]
        forward.append((count - 1, 0))
        backward = [(target, source) for source, target in forward]
        low = lax.ppermute(
            lax.slice_in_dim(block, block.shape[dim] - width, None, axis=dim), axis, forward
        )
        high = lax.ppermute(lax.slice_in_dim(block, 0, width, axis=dim), axis, backward)
        block = jnp.concatenate([low, block, high], axis=dim)
    return block


def fraction_weights(sample_abscissae, singularity_locations, basis_normalizers, spectral_target):
    gap_real = spectral_target[0] - sample_abscissae[:, 0]
    gap_imag = spectral_target[1] - sample_abscissae[:, 1]
    pole_size = (
        singularity_locations[:, 0] * singularity_locations[:, 0]
        + singularity_locations[:, 1] * singularity_locations[:, 1]
    )
    quotient_inphase = (
        spectral_target[0] * singularity_locations[:, 0]
        + spectral_target[1] * singularity_locations[:, 1]
    ) / pole_size
    quotient_quadrature = (
        spectral_target[1] * singularity_locations[:, 0]
        - spectral_target[0] * singularity_locations[:, 1]
    ) / pole_size
    subordinate_inphase = basis_normalizers * (1.0 - quotient_inphase)
    subordinate_quadrature = -basis_normalizers * quotient_quadrature
    lower_size = (
        subordinate_inphase * subordinate_inphase + subordinate_quadrature * subordinate_quadrature
    )
    multiplier_inphase = (
        gap_real * subordinate_inphase + gap_imag * subordinate_quadrature
    ) / lower_size
    multiplier_quadrature = (
        gap_imag * subordinate_inphase - gap_real * subordinate_quadrature
    ) / lower_size
    return (multiplier_inphase, multiplier_quadrature)


def cell_inverse(onehot, principal_entry_addend):
    shifted = jnp.einsum("mxy,mc->cxy", onehot, principal_entry_addend, precision=HIGHEST)
    center = 4.0 + shifted[0]
    size_sq = center * center + shifted[1] * shifted[1]
    return jnp.stack([center / size_sq, -shifted[1] / size_sq])


def times_inverse(grid_field, inverse):
    real_part = grid_field[:, 0] * inverse[0] - grid_field[:, 1] * inverse[1]
    imag_part = grid_field[:, 0] * inverse[1] + grid_field[:, 1] * inverse[0]
    return jnp.stack([real_part, imag_part], 1)


def neighbours(padded):
    return (
        padded[:, :, 2:, 1:-1]
        + padded[:, :, :-2, 1:-1]
        + padded[:, :, 1:-1, 2:]
        + padded[:, :, 1:-1, :-2]
    )


def rotate(padded, angles, row_sign, column_sign):
    phase_angle = (
        row_sign[None, :, None] * angles[:, 0][:, None, None]
        + column_sign[None, None, :] * angles[:, 1][:, None, None]
    )
    cosine = jnp.cos(phase_angle)
    sine_part = jnp.sin(phase_angle)
    real_part = padded[:, 0] * cosine - padded[:, 1] * sine_part
    imag_part = padded[:, 0] * sine_part + padded[:, 1] * cosine
    return jnp.stack([real_part, imag_part], 1)


def body_twist(padded, angles, margin):
    row_count = padded.shape[2]
    column_count = padded.shape[3]
    row_positions = jnp.arange(row_count)
    column_positions = jnp.arange(column_count)
    low_rows = lax.axis_index("gx") == 0
    high_rows = lax.axis_index("gx") == lax.axis_size("gx") - 1
    low_columns = lax.axis_index("gy") == 0
    high_columns = lax.axis_index("gy") == lax.axis_size("gy") - 1
    row_sign = jnp.where(low_rows & (row_positions < margin), -1.0, 0.0) + jnp.where(
        high_rows & (row_positions >= row_count - margin), 1.0, 0.0
    )
    column_sign = jnp.where(low_columns & (column_positions < margin), -1.0, 0.0) + jnp.where(
        high_columns & (column_positions >= column_count - margin), 1.0, 0.0
    )
    return rotate(padded, angles, row_sign.astype(jnp.float32), column_sign.astype(jnp.float32))


def right_side(vectors_now, current, linearized_block_weight, onehot):
    mixing_real = jnp.einsum(
        "bm,kbc->kmc", linearized_block_weight[:, :, 0], current[:, :, 0], precision=HIGHEST
    ) - jnp.einsum(
        "bm,kbc->kmc", linearized_block_weight[:, :, 1], current[:, :, 1], precision=HIGHEST
    )
    mixing_imag = jnp.einsum(
        "bm,kbc->kmc", linearized_block_weight[:, :, 0], current[:, :, 1], precision=HIGHEST
    ) + jnp.einsum(
        "bm,kbc->kmc", linearized_block_weight[:, :, 1], current[:, :, 0], precision=HIGHEST
    )
    cell_real = jnp.einsum("kmc,mxy->kcxy", mixing_real, onehot, precision=HIGHEST)
    cell_imag = jnp.einsum("kmc,mxy->kcxy", mixing_imag, onehot, precision=HIGHEST)
    real_part = jnp.sum(cell_real * vectors_now[:, :, 0] - cell_imag * vectors_now[:, :, 1], axis=1)
    imag_part = jnp.sum(cell_real * vectors_now[:, :, 1] + cell_imag * vectors_now[:, :, 0], axis=1)
    return jnp.stack([real_part, imag_part], 1)


def grid_inner(vectors_now, grid_field):
    inner_real = jnp.einsum(
        "kcxy,kxy->kc", vectors_now[:, :, 0], grid_field[:, 0], precision=HIGHEST
    ) + jnp.einsum("kcxy,kxy->kc", vectors_now[:, :, 1], grid_field[:, 1], precision=HIGHEST)
    inner_imag = jnp.einsum(
        "kcxy,kxy->kc", vectors_now[:, :, 0], grid_field[:, 1], precision=HIGHEST
    ) - jnp.einsum("kcxy,kxy->kc", vectors_now[:, :, 1], grid_field[:, 0], precision=HIGHEST)
    return (inner_real, inner_imag)


def grid_remove(vectors_now, grid_field, inner_real, inner_imag):
    real_part = grid_field[:, 0] - (
        jnp.einsum("kc,kcxy->kxy", inner_real, vectors_now[:, :, 0], precision=HIGHEST)
        - jnp.einsum("kc,kcxy->kxy", inner_imag, vectors_now[:, :, 1], precision=HIGHEST)
    )
    imag_part = grid_field[:, 1] - (
        jnp.einsum("kc,kcxy->kxy", inner_real, vectors_now[:, :, 1], precision=HIGHEST)
        + jnp.einsum("kc,kcxy->kxy", inner_imag, vectors_now[:, :, 0], precision=HIGHEST)
    )
    return jnp.stack([real_part, imag_part], 1)


def block_chain(coords_real, coords_imag, current_full, multiplier_inphase, multiplier_quadrature):
    blockwise = [jnp.stack([coords_real, coords_imag], 1)]
    for block_id in range(current_full.shape[1] - 1):
        previous = blockwise[-1]
        real_part = (
            multiplier_inphase[block_id] * previous[:, 0]
            - multiplier_quadrature[block_id] * previous[:, 1]
            + current_full[:, block_id + 1, 0]
        )
        imag_part = (
            multiplier_inphase[block_id] * previous[:, 1]
            + multiplier_quadrature[block_id] * previous[:, 0]
            + current_full[:, block_id + 1, 1]
        )
        blockwise.append(jnp.stack([real_part, imag_part], 1))
    return jnp.stack(blockwise, 1)


def level_inner(older, newer):
    inner_real = jnp.einsum(
        "kcbr,kbr->kc", older[:, :, :, 0], newer[:, :, 0], precision=HIGHEST
    ) + jnp.einsum("kcbr,kbr->kc", older[:, :, :, 1], newer[:, :, 1], precision=HIGHEST)
    inner_imag = jnp.einsum(
        "kcbr,kbr->kc", older[:, :, :, 0], newer[:, :, 1], precision=HIGHEST
    ) - jnp.einsum("kcbr,kbr->kc", older[:, :, :, 1], newer[:, :, 0], precision=HIGHEST)
    return (inner_real, inner_imag)


def level_remove(older, newer, inner_real, inner_imag):
    real_part = newer[:, :, 0] - (
        jnp.einsum("kc,kcbr->kbr", inner_real, older[:, :, :, 0], precision=HIGHEST)
        - jnp.einsum("kc,kcbr->kbr", inner_imag, older[:, :, :, 1], precision=HIGHEST)
    )
    imag_part = newer[:, :, 1] - (
        jnp.einsum("kc,kcbr->kbr", inner_real, older[:, :, :, 1], precision=HIGHEST)
        + jnp.einsum("kc,kcbr->kbr", inner_imag, older[:, :, :, 0], precision=HIGHEST)
    )
    return jnp.stack([real_part, imag_part], 2)


def level_step(coeffs, hessen, blockwise, active, section_id):
    older = coeffs[:, :active]
    first_real, first_imag = level_inner(older, blockwise)
    orthog_once = level_remove(older, blockwise, first_real, first_imag)
    second_real, second_imag = level_inner(older, orthog_once)
    orthog_twice = level_remove(older, orthog_once, second_real, second_imag)
    length = jnp.sqrt(jnp.sum(orthog_twice * orthog_twice, axis=(1, 2, 3)))
    coeffs = coeffs.at[:, active].set(orthog_twice / length[:, None, None, None])
    hessen = hessen.at[:, 0, :active, section_id].set(first_real + second_real)
    hessen = hessen.at[:, 1, :active, section_id].set(first_imag + second_imag)
    hessen = hessen.at[:, 0, active, section_id].set(length)
    return (coeffs, hessen)


def per_device(
    initial_guess_field,
    medium_label,
    principal_entry_addend,
    linearized_block_weight,
    sample_abscissae,
    singularity_locations,
    basis_normalizers,
    spectral_target,
    quasi_periodic_phase,
):
    materials = principal_entry_addend.shape[0]
    points = initial_guess_field.shape[0]
    blocks = linearized_block_weight.shape[0]
    rank_count = STEPS + 1
    onehot = (medium_label[None] == jnp.arange(materials, dtype=jnp.int32)[:, None, None]).astype(
        jnp.float32
    )
    inverse = cell_inverse(onehot, principal_entry_addend)
    multiplier_inphase, multiplier_quadrature = fraction_weights(
        sample_abscissae, singularity_locations, basis_normalizers, spectral_target
    )
    squares = jnp.sum(initial_guess_field * initial_guess_field, axis=(1, 2, 3))
    scale_start = jnp.sqrt(lax.psum(squares, ("gx", "gy")))
    vectors = [initial_guess_field / scale_start[:, None, None, None]]
    coeffs = (
        jnp.zeros((points, rank_count, blocks, 2, rank_count), jnp.float32)
        .at[:, 0, 0, 0, 0]
        .set(1.0)
    )
    hessen = jnp.zeros((points, 2, rank_count, STEPS), jnp.float32)
    for section_id in range(STEPS):
        active = section_id + 1
        vectors_now = jnp.stack(vectors, 1)
        source = right_side(
            vectors_now, coeffs[:, section_id, :, :, :active], linearized_block_weight, onehot
        )
        solved = times_inverse(source, inverse)
        for repeat in range(SWEEPS):
            padded = padded_2(solved, (("gx", 2), ("gy", 3)), 1)
            padded = body_twist(padded, quasi_periodic_phase, 1)
            solved = times_inverse(source + neighbours(padded), inverse)
        part_real, part_imag = grid_inner(vectors_now, solved)
        part_square = jnp.sum(solved * solved, axis=(1, 2, 3))
        inner_real, inner_imag, whole_square = lax.psum(
            (part_real, part_imag, part_square), ("gx", "gy")
        )
        orthog_once = grid_remove(vectors_now, solved, inner_real, inner_imag)
        length = jnp.sqrt(
            whole_square - jnp.sum(inner_real * inner_real + inner_imag * inner_imag, axis=1)
        )
        vectors.append(orthog_once / length[:, None, None, None])
        coords_real = (
            jnp.zeros((points, rank_count), jnp.float32)
            .at[:, :active]
            .set(inner_real)
            .at[:, active]
            .set(length)
        )
        coords_imag = jnp.zeros((points, rank_count), jnp.float32).at[:, :active].set(inner_imag)
        blockwise = block_chain(
            coords_real,
            coords_imag,
            coeffs[:, section_id],
            multiplier_inphase,
            multiplier_quadrature,
        )
        coeffs, hessen = level_step(coeffs, hessen, blockwise, active, section_id)
    return (jnp.stack(vectors[1:], 1), hessen)


def solution(mesh):
    return jax.shard_map(
        per_device,
        mesh=mesh,
        in_specs=(P(None, None, "gx", "gy"), P("gx", "gy"), P(), P(), P(), P(), P(), P(), P()),
        out_specs=(P(None, None, None, "gx", "gy"), P()),
        check_vma=False,
    )
```

profile of v0, /device:TPU:14, one launch (start us, length us, event | category | flops | bytes accessed | tf_op | source)
XLA Modules:
  0.0 701.8 jit_solution(3626380374497232272)
XLA Ops:
  7.6 40.2 %psum.70 = f32[2]{0:T(128)S(1)} all-reduce(f32[2]{0:T(128)S(1)} %multiply_reduce_fusion), channel_id=1, replica_groups=mesh['gx'=8,'gy'=4] {'gx','gy'}, use_global_device_ids=true, to_apply=%region_1.0 | all-reduce | flops 2 | bytes 16 | tf_op jit(solution)/shard_map/psum | solution.py:223
  59.1 3.5 collective-permute-done.2
  63.5 5.5 fusion.165
  82.7 5.5 fusion.167
  103.5 5.5 fusion.169
  125.1 5.5 fusion.171
  135.8 43.1 %all-reduce.8 = (f32[2,1]{0,1:T(1,128)S(1)}, f32[2,1]{0,1:T(1,128)S(1)}, f32[2]{0:T(128)S(1)}) all-reduce(f32[2,1]{0,1:T(1,128)S(1)} %subtract_bitcast_fusion.5, f32[2,1]{0,1:T(1,128)S(1)} %add_bitcast_fusion.7, f32[2]{0:T(128)S(1)} %fusion.109), channel_id=1, replica_groups=mesh['gx'=8,'gy'=4] {'gx','gy'}, use_global_device_ids=true, to_apply=%region_3.0 | all-reduce | flops 6 | bytes 48 | tf_op jit(solution)/shard_map/psum | solution.py:244
  181.0 29.7 %multiply_subtract_fusion.15 = (f32[2,4]{0,1:T(4,128)S(1)}, f32[2,4]{0,1:T(4,128)S(1)}, f32[2,4]{0,1:T(4,128)S(1)}, f32[2,4]{0,1:T(4,128)S(1)}, f32[2,4]{0,1:T(4...) fusion(f32[]{:T(128)} %bitcast.148, ...), kind=kLoop, calls=%fused_computation.778 | loop fusion | flops 1128 | bytes 1736 | tf_op jit(solution)/shard_map/sub | solution.py:151
  233.6 3.2 collective-permute-done.18
  237.8 5.5 fusion.173
  252.7 3.4 collective-permute-done.22
  257.0 5.5 fusion.175
  272.5 3.9 collective-permute-done.26
  277.3 5.5 fusion.177
  299.1 5.5 fusion.179
  308.1 4.9 fusion.219
  313.0 4.9 fusion.215
  317.9 4.9 fusion.211
  322.8 5.3 fusion.209
  329.2 44.7 %all-reduce.7 = (f32[2,2]{0,1:T(2,128)S(1)}, f32[2,2]{0,1:T(2,128)S(1)}, f32[2]{0:T(128)S(1)}) all-reduce(f32[2,2]{0,1:T(2,128)S(1)} %bitcast_subtract_fusion.7, f32[2,2]{0,1:T(2,128)S(1)} %bitcast_add_fusion.99, f32[2]{0:T(128)S(1)} %fusion.110), channel_id=1, replica_groups=mesh['gx'=8,'gy'=4] {'gx','gy'}, use_global_device_ids=true, to_apply=%region_12.13 | all-reduce | flops 10 | bytes 80 | tf_op jit(solution)/shard_map/psum | solution.py:244
  375.5 29.8 %bitcast_add_fusion.52 = (f32[2,4]{0,1:T(4,128)S(1)}, f32[2,4]{0,1:T(4,128)S(1)}, f32[2,4]{0,1:T(4,128)S(1)}, f32[2,4]{0,1:T(4,128)S(1)}, f32[2,4]{0,1:T(4,128)S...) fusion(f32[2,1,1,4]{0,3,2,1:T(4,128)S(1)} %copy.2232, ...), kind=kLoop, calls=%fused_computation.729 | loop fusion | flops 1504 | bytes 3248 | tf_op jit(solution)/shard_map/add | solution.py:151
  449.5 5.5 fusion.181
  469.0 5.5 fusion.183
  485.0 3.4 collective-permute-done.42
  489.2 5.5 fusion.185
  567.4 5.5 fusion.187
  576.3 4.9 fusion.20
  581.2 4.9 fusion.16
  586.1 4.9 fusion.12
  591.4 5.0 fusion.10
  598.1 45.0 %all-reduce.6 = (f32[2,3]{0,1:T(4,128)S(1)}, f32[2,3]{0,1:T(4,128)S(1)}, f32[2]{0:T(128)S(1)}) all-reduce(f32[2,3]{0,1:T(4,128)S(1)} %bitcast_subtract_fusion.6, f32[2,3]{0,1:T(4,128)S(1)} %bitcast_add_fusion.50, f32[2]{0:T(128)S(1)} %fusion.111), channel_id=1, replica_groups=mesh['gx'=8,'gy'=4] {'gx','gy'}, use_global_device_ids=true, to_apply=%region_22.23 | all-reduce | flops 14 | bytes 112 | tf_op jit(solution)/shard_map/psum | solution.py:244
  643.7 29.8 %bitcast_add_fusion.3 = (f32[2,4]{0,1:T(4,128)S(1)}, f32[2,4]{0,1:T(4,128)S(1)}, f32[2,4]{0,1:T(4,128)S(1)}, f32[2,4]{0,1:T(4,128)S(1)}, f32[2,4]{0,1:T(4,128)S(...) fusion(f32[2,1,1,4]{0,3,2,1:T(4,128)S(1)} %copy-done.46, ...), kind=kLoop, calls=%fused_computation.679 | loop fusion | flops 1512 | bytes 3288 | tf_op jit(solution)/shard_map/add | solution.py:151
  (888 shorter events, 313.2 us)
Async XLA Ops:
  56.7 5.9 collective-permute-start.2
  56.8 5.8 collective-permute-start.3
  71.7 4.6 collective-permute-start.5
  76.6 5.3 collective-permute-start.6
  76.6 5.2 collective-permute-start.7
  91.3 5.3 collective-permute-start.9
  96.9 5.7 collective-permute-start.10
  96.9 5.7 collective-permute-start.11
  118.5 5.7 collective-permute-start.14
  118.5 5.7 collective-permute-start.15
  231.3 5.5 collective-permute-start.18
  231.4 5.4 collective-permute-start.19
  250.8 5.3 collective-permute-start.22
  250.8 5.3 collective-permute-start.23
  265.2 5.1 collective-permute-start.25
  270.6 5.8 collective-permute-start.26
  270.6 5.8 collective-permute-start.27
  285.4 6.4 collective-permute-start.28
  292.3 5.9 collective-permute-start.30
  292.3 5.8 collective-permute-start.31
  442.7 5.9 collective-permute-start.34
  442.8 5.8 collective-permute-start.35
  457.7 4.6 collective-permute-start.37
  462.5 5.6 collective-permute-start.38
  462.6 5.5 collective-permute-start.39
  477.2 5.0 collective-permute-start.41
  482.4 5.9 collective-permute-start.42
  482.5 5.8 collective-permute-start.43
  498.7 52.7 %collective-permute-start.44 = (f32[2,2,1,512]{3,0,2,1:T(2,128)}, f32[2,2,1,512]{3,0,2,1:T(2,128)S(1)}, u32[]{:S(2)}, u32[]{:S(2)}) collective-permute-start(f32[2,2,1,512]{3,0,2,1:T(2,128)} %get-tuple-element.559), channel_id=1, source_target_pairs={{0,4},{4,8},{8,12},{12,16},{16,20},{20,24},{24,28},{28,0},{1,5},{5... | collective-permute-start | bytes 24584 | tf_op jit(solution)/shard_map/ppermute | solution.py:17
  500.7 50.7 %collective-permute-start.45 = (f32[2,2,1,512]{3,0,2,1:T(2,128)}, f32[2,2,1,512]{3,0,2,1:T(2,128)S(1)}, u32[]{:S(2)}, u32[]{:S(2)}) collective-permute-start(f32[2,2,1,512]{3,0,2,1:T(2,128)} %get-tuple-element.560), channel_id=1, source_target_pairs={{4,0},{8,4},{12,8},{16,12},{20,16},{24,20},{28,24},{0,28},{5,1},{9... | collective-permute-start | bytes 24584 | tf_op jit(solution)/shard_map/ppermute | solution.py:20
  553.2 12.2 %collective-permute-start.46 = (f32[2,2,66,1]{3,0,2,1:T(2,128)}, f32[2,2,66,1]{3,0,2,1:T(2,128)}, u32[]{:S(2)}, u32[]{:S(2)}) collective-permute-start(f32[2,2,66,1]{3,0,2,1:T(2,128)} %get-tuple-element.533), channel_id=1, source_target_pairs={{0,1},{1,2},{2,3},{3,0},{4,5},{5,6},{6,7},{7,4},{8,9},{9,10},{10,1... | collective-permute-start | bytes 3176 | tf_op jit(solution)/shard_map/ppermute | solution.py:17
  553.2 12.2 %collective-permute-start.47 = (f32[2,2,66,1]{3,0,2,1:T(2,128)}, f32[2,2,66,1]{3,0,2,1:T(2,128)}, u32[]{:S(2)}, u32[]{:S(2)}) collective-permute-start(f32[2,2,66,1]{3,0,2,1:T(2,128)} %get-tuple-element.534), channel_id=1, source_target_pairs={{1,0},{2,1},{3,2},{0,3},{5,4},{6,5},{7,6},{4,7},{9,8},{10,9},{11,1... | collective-permute-start | bytes 3176 | tf_op jit(solution)/shard_map/ppermute | solution.py:20
  (82 other events, 2453.6 us)
where the time goes:
time: 712 us; the launch traced here: 702 us
  other arithmetic  231 us (32%)
  blocking collectives  173 us (24%)
  local copies, waits for them, and re-layouts  103 us (14%)
  matrix products  80.5 us (11%)
  waiting for transfers between devices  62.5 us (9%)
  starting transfers between devices  48.4 us (7%)
    psum x3, blocking collectives, per_device(): lax.psum((part_real, part_imag, part_square), ('gx', 'gy'))  133 us
    add x12, other arithmetic, rotate(): imag_part = padded[:, 0] * sine_part + padded[:, 1] * cosine  65.8 us
    add x2, other arithmetic, block_chain(): multiplier_inphase[block_id] * previous[:, 0]  59.6 us
    ppermute x24, waiting for transfers between devices, padded_2(): lax.ppermute(lax.slice_in_dim(block, block.shape[dim] - width, None, axis...  43 us
    psum x1, blocking collectives, per_device(): scale_start = jnp.sqrt(lax.psum(squares, ('gx', 'gy')))  40.2 us
    ppermute x24, starting transfers between devices, padded_2(): lax.ppermute(lax.slice_in_dim(block, 0, width, axis=dim), axis, backward)  34.5 us
    squeeze x48, local copies, waits for them, and re-layouts, block_chain(): current_full[:, block_id + 1, 0]  33.2 us
    squeeze x48, local copies, waits for them, and re-layouts, block_chain(): current_full[:, block_id + 1, 1]  31.5 us
  transfers between devices with their start and end apart: 48, of which 31 were waited for; matrix products, arithmetic and copies ran while one was open for 11% of the time, Pallas kernels for 0%

commit v1 on v0

--- a/solution.py
+++ b/solution.py
@@ -242,7 +242,7 @@
         part_real, part_imag = grid_inner(vectors_now, solved)
         part_square = jnp.sum(solved * solved, axis=(1, 2, 3))
         inner_real, inner_imag, whole_square = lax.psum(
-            (part_real, part_imag, part_square), ("gx", "gy")
+            lax.psum((part_real, part_imag, part_square), "gx"), "gy"
         )
         orthog_once = grid_remove(vectors_now, solved, inner_real, inner_imag)
         length = jnp.sqrt(

time: 712 us -> 673 us (0.945)
  the two profiles are of different devices: /device:TPU:14 before, /device:TPU:0 now
where the time goes in v1:
time: 673 us; the launch traced here: 663 us
  other arithmetic  231 us (34%)
  blocking collectives  120 us (18%)
  local copies, waits for them, and re-layouts  103 us (15%)
  starting transfers between devices  80.9 us (12%)
  matrix products  80.3 us (12%)
  waiting for transfers between devices  44 us (7%)
    ppermute x24, starting transfers between devices, padded_2(): lax.ppermute(lax.slice_in_dim(block, 0, width, axis=dim), axis, backward)  71.1 us
    add x12, other arithmetic, rotate(): imag_part = padded[:, 0] * sine_part + padded[:, 1] * cosine  65.8 us
    psum x3, blocking collectives, per_device(): lax.psum((part_real, part_imag, part_square), 'gx')  59.9 us
    add x2, other arithmetic, block_chain(): multiplier_inphase[block_id] * previous[:, 0]  59.6 us
    psum x1, blocking collectives, per_device(): scale_start = jnp.sqrt(lax.psum(squares, ('gx', 'gy')))  41.9 us
    squeeze x48, local copies, waits for them, and re-layouts, block_chain(): current_full[:, block_id + 1, 0]  33.2 us
    squeeze x48, local copies, waits for them, and re-layouts, block_chain(): current_full[:, block_id + 1, 1]  31.7 us
    ppermute x24, waiting for transfers between devices, padded_2(): lax.ppermute(lax.slice_in_dim(block, block.shape[dim] - width, None, axis...  30 us
  transfers between devices with their start and end apart: 48, of which 32 were waited for; matrix products, arithmetic and copies ran while one was open for 12% of the time, Pallas kernels for 0%

profile of v1, /device:TPU:0, one launch (start us, length us, event | category | flops | bytes accessed | tf_op | source)
XLA Modules:
  0.0 662.9 jit_solution(6838662646854023378)
XLA Ops:
  7.6 41.9 %psum.133 = f32[2]{0:T(128)S(1)} all-reduce(f32[2]{0:T(128)S(1)} %multiply_reduce_fusion), channel_id=1, replica_groups=mesh['gx'=8,'gy'=4] {'gx','gy'}, use_global_device_ids=true, to_apply=%region_1.0 | all-reduce | flops 2 | bytes 16 | tf_op jit(solution)/shard_map/psum | solution.py:223
  64.6 5.5 fusion.165
  86.2 5.5 fusion.167
  94.4 4.8 collective-permute-start.9
  107.6 5.5 fusion.169
  115.8 4.8 collective-permute-start.13
  129.3 5.5 fusion.171
  140.0 21.9 %all-reduce.8 = (f32[2,1]{0,1:T(1,128)S(1)}, f32[2,1]{0,1:T(1,128)S(1)}, f32[2]{0:T(128)S(1)}) all-reduce(f32[2,1]{0,1:T(1,128)S(1)} %subtract_bitcast_fusion.5, f32[2,1]{0,1:T(1,128)S(1)} %add_bitcast_fusion.7, f32[2]{0:T(128)S(1)} %fusion.109), channel_id=1, replica_groups=mesh['gx'=8,'gy'=4] {'gx'}, use_global_device_ids=true, to_apply=%region_4.0 | all-reduce | flops 6 | bytes 48 | tf_op jit(solution)/shard_map/psum | solution.py:245
  161.9 5.9 all-reduce.11
  169.8 29.8 %multiply_subtract_fusion.15 = (f32[2,4]{0,1:T(4,128)S(1)}, f32[2,4]{0,1:T(4,128)S(1)}, f32[2,4]{0,1:T(4,128)S(1)}, f32[2,4]{0,1:T(4,128)S(1)}, f32[2,4]{0,1:T(4...) fusion(f32[]{:T(128)} %bitcast.148, ...), kind=kLoop, calls=%fused_computation.778 | loop fusion | flops 1128 | bytes 1736 | tf_op jit(solution)/shard_map/sub | solution.py:151
  225.9 5.5 fusion.173
  247.2 5.5 fusion.175
  268.7 5.5 fusion.177
  293.1 5.5 fusion.179
  302.4 4.9 fusion.219
  307.3 4.9 fusion.215
  312.2 4.9 fusion.211
  317.1 5.1 fusion.209
  323.2 18.7 %all-reduce.7 = (f32[2,2]{0,1:T(2,128)S(1)}, f32[2,2]{0,1:T(2,128)S(1)}, f32[2]{0:T(128)S(1)}) all-reduce(f32[2,2]{0,1:T(2,128)S(1)} %bitcast_subtract_fusion.7, f32[2,2]{0,1:T(2,128)S(1)} %bitcast_add_fusion.99, f32[2]{0:T(128)S(1)} %fusion.110), channel_id=1, replica_groups=mesh['gx'=8,'gy'=4] {'gx'}, use_global_device_ids=true, to_apply=%region_16.17 | all-reduce | flops 10 | bytes 80 | tf_op jit(solution)/shard_map/psum | solution.py:245
  341.9 6.3 all-reduce.10
  349.7 29.8 %bitcast_add_fusion.52 = (f32[2,4]{0,1:T(4,128)S(1)}, f32[2,4]{0,1:T(4,128)S(1)}, f32[2,4]{0,1:T(4,128)S(1)}, f32[2,4]{0,1:T(4,128)S(1)}, f32[2,4]{0,1:T(4,128)S...) fusion(f32[2,1,1,4]{0,3,2,1:T(4,128)S(1)} %copy.2232, ...), kind=kLoop, calls=%fused_computation.729 | loop fusion | flops 1504 | bytes 3248 | tf_op jit(solution)/shard_map/add | solution.py:151
  424.3 5.5 fusion.181
  445.7 5.5 fusion.183
  467.1 5.5 fusion.185
  548.1 5.5 fusion.187
  556.7 4.9 fusion.20
  561.6 4.9 fusion.16
  566.5 4.9 fusion.12
  571.8 5.1 fusion.10
  578.6 19.4 %all-reduce.6 = (f32[2,3]{0,1:T(4,128)S(1)}, f32[2,3]{0,1:T(4,128)S(1)}, f32[2]{0:T(128)S(1)}) all-reduce(f32[2,3]{0,1:T(4,128)S(1)} %bitcast_subtract_fusion.6, f32[2,3]{0,1:T(4,128)S(1)} %bitcast_add_fusion.50, f32[2]{0:T(128)S(1)} %fusion.111), channel_id=1, replica_groups=mesh['gx'=8,'gy'=4] {'gx'}, use_global_device_ids=true, to_apply=%region_29.30 | all-reduce | flops 14 | bytes 112 | tf_op jit(solution)/shard_map/psum | solution.py:245
  598.0 5.9 all-reduce.9
  604.4 29.8 %bitcast_add_fusion.3 = (f32[2,4]{0,1:T(4,128)S(1)}, f32[2,4]{0,1:T(4,128)S(1)}, f32[2,4]{0,1:T(4,128)S(1)}, f32[2,4]{0,1:T(4,128)S(1)}, f32[2,4]{0,1:T(4,128)S(...) fusion(f32[2,1,1,4]{0,3,2,1:T(4,128)S(1)} %copy-done.46, ...), kind=kLoop, calls=%fused_computation.679 | loop fusion | flops 1512 | bytes 3288 | tf_op jit(solution)/shard_map/add | solution.py:151
  (891 shorter events, 335.2 us)
Async XLA Ops:
  51.4 6.4 collective-permute-start
  58.0 5.7 collective-permute-start.3
  72.8 6.4 collective-permute-start.4
  80.1 5.2 collective-permute-start.7
  94.3 6.5 collective-permute-start.8
  94.4 6.4 collective-permute-start.9
  101.5 5.2 collective-permute-start.11
  115.8 6.5 collective-permute-start.12
  115.8 6.4 collective-permute-start.13
  122.9 5.6 collective-permute-start.15
  212.7 6.4 collective-permute-start.16
  212.8 6.3 collective-permute-start.17
  219.4 5.6 collective-permute-start.19
  234.0 6.4 collective-permute-start.20
  234.1 6.3 collective-permute-start.21
  255.4 6.5 collective-permute-start.24
  255.4 6.4 collective-permute-start.25
  262.4 5.4 collective-permute-start.27
  276.8 9.2 %collective-permute-start.28 = (f32[2,2,1,512]{3,0,2,1:T(2,128)S(1)}, f32[2,2,1,512]{3,0,2,1:T(2,128)S(1)}, u32[]{:S(2)}, u32[]{:S(2)}) collective-permute-start(f32[2,2,1,512]{3,0,2,1:T(2,128)S(1)} %get-tuple-element.576), channel_id=1, source_target_pairs={{0,4},{4,8},{8,12},{12,16},{16,20},{20,24},{24,28},{28,0},{1,5},{5... | collective-permute-start | bytes 24584 | tf_op jit(solution)/shard_map/ppermute | solution.py:17
  276.9 9.1 %collective-permute-start.29 = (f32[2,2,1,512]{3,0,2,1:T(2,128)S(1)}, f32[2,2,1,512]{3,0,2,1:T(2,128)S(1)}, u32[]{:S(2)}, u32[]{:S(2)}) collective-permute-start(f32[2,2,1,512]{3,0,2,1:T(2,128)S(1)} %get-tuple-element.577), channel_id=1, source_target_pairs={{4,0},{8,4},{12,8},{16,12},{20,16},{24,20},{28,24},{0,28},{5,1},{9... | collective-permute-start | bytes 24584 | tf_op jit(solution)/shard_map/ppermute | solution.py:20
  411.1 6.4 collective-permute-start.32
  411.3 6.2 collective-permute-start.33
  417.8 5.6 collective-permute-start.35
  432.4 6.4 collective-permute-start.36
  432.5 6.3 collective-permute-start.37
  439.4 5.5 collective-permute-start.39
  453.9 6.5 collective-permute-start.40
  453.9 6.4 collective-permute-start.41
  476.5 55.6 %collective-permute-start.44 = (f32[2,2,1,512]{3,0,2,1:T(2,128)}, f32[2,2,1,512]{3,0,2,1:T(2,128)S(1)}, u32[]{:S(2)}, u32[]{:S(2)}) collective-permute-start(f32[2,2,1,512]{3,0,2,1:T(2,128)} %get-tuple-element.568), channel_id=1, source_target_pairs={{0,4},{4,8},{8,12},{12,16},{16,20},{20,24},{24,28},{28,0},{1,5},{5... | collective-permute-start | bytes 24584 | tf_op jit(solution)/shard_map/ppermute | solution.py:17
  476.5 55.6 %collective-permute-start.45 = (f32[2,2,1,512]{3,0,2,1:T(2,128)}, f32[2,2,1,512]{3,0,2,1:T(2,128)S(1)}, u32[]{:S(2)}, u32[]{:S(2)}) collective-permute-start(f32[2,2,1,512]{3,0,2,1:T(2,128)} %get-tuple-element.569), channel_id=1, source_target_pairs={{4,0},{8,4},{12,8},{16,12},{20,16},{24,20},{28,24},{0,28},{5,1},{9... | collective-permute-start | bytes 24584 | tf_op jit(solution)/shard_map/ppermute | solution.py:20
  533.9 12.1 %collective-permute-start.46 = (f32[2,2,66,1]{3,0,2,1:T(2,128)}, f32[2,2,66,1]{3,0,2,1:T(2,128)}, u32[]{:S(2)}, u32[]{:S(2)}) collective-permute-start(f32[2,2,66,1]{3,0,2,1:T(2,128)} %get-tuple-element.542), channel_id=1, source_target_pairs={{0,1},{1,2},{2,3},{3,0},{4,5},{5,6},{6,7},{7,4},{8,9},{9,10},{10,1... | collective-permute-start | bytes 3176 | tf_op jit(solution)/shard_map/ppermute | solution.py:17
  534.8 11.3 %collective-permute-start.47 = (f32[2,2,66,1]{3,0,2,1:T(2,128)}, f32[2,2,66,1]{3,0,2,1:T(2,128)}, u32[]{:S(2)}, u32[]{:S(2)}) collective-permute-start(f32[2,2,66,1]{3,0,2,1:T(2,128)} %get-tuple-element.543), channel_id=1, source_target_pairs={{1,0},{2,1},{3,2},{0,3},{5,4},{6,5},{7,6},{4,7},{9,8},{10,9},{11,1... | collective-permute-start | bytes 3176 | tf_op jit(solution)/shard_map/ppermute | solution.py:20
  (82 other events, 1678.3 us)
